TPU v7x, 32 devices: a whole 2x2x4 slice. The times are simulated.
32 devices in a mesh: ctx: 8 (over z, y), tp: 4 (over x, core).
Axes of the slice: x: 2, y: 2, z: 4, core: 2. Of those that a mesh axis runs over, the one named last changes fastest.
Arguments:
- stream_in: float32 [3072, 2048], P('ctx'), may hold values from -6 to 6
- cotangent: float32 [3072, 2048], P('ctx'), may hold values from -6 to 6
- ln_gain: float32 [2, 2048], replicated, may hold values from 0.5 to 1.5
- ln_bias: float32 [2, 2048], replicated, may hold values from -3 to 3
- w_qkv: bfloat16 [2048, 6144], P(None, 'tp'), may hold values from -0.46403883 to 0.46403883
- b_qkv: float32 [6144], P('tp'), may hold values from -1 to 1
- w_out: bfloat16 [2048, 2048], P('tp'), may hold values from -0.5 to 0.5
- out_bias: float32 [2048], replicated, may hold values from -3 to 3
- w_up: bfloat16 [2048, 8192], P(None, 'tp'), may hold values from -0.125 to 0.125
- b_up: float32 [8192], P('tp'), may hold values from -3 to 3
- w_down: bfloat16 [8192, 2048], P('tp'), may hold values from -0.0625 to 0.0625
- block_order: int32 [16], replicated, may hold values from 0 to 15, as said below
Outputs:
- stream_out: float32 [3072, 2048], P('ctx')
- grad_in: float32 [3072, 2048], P('ctx')
- grad_w_qkv: float32 [2048, 6144], P('ctx', 'tp')
- grad_b_qkv: float32 [6144], P('tp')
- grad_w_out: float32 [2048, 2048], P('tp', 'ctx')
- grad_out_bias: float32 [2048], replicated
- grad_w_up: float32 [2048, 8192], P('ctx', 'tp')
- grad_b_up: float32 [8192], P('tp')
- grad_w_down: float32 [8192, 2048], P('tp', 'ctx')
- grad_ln_gain: float32 [2, 2048], replicated
- grad_ln_bias: float32 [2, 2048], replicated
Inputs may be any that keep to these rules, and one draw needn't show every extreme that they name: `block_order`: entries 2 d and 2 d + 1 are b and 15 - b for some b; each value appears once.
All inputs are finite; a program needn't handle non-finite values.
Results may differ from a plain program's by a relative error of at most 0.04.
Values may be sent and summed in bfloat16 or wider, within the bound.
A program may use at most 384 MiB of HBM per device.

v0:
```python
import math
import jax
import jax.numpy as jnp
from jax import lax
from jax.sharding import PartitionSpec as P

HD = 256
ROT = 64
masked_value = -1e30
norm_epsilon = 1e-05
root_half = 0.7071067811865476
inverse_root_two_pi = 0.3989422804014327


def stored_positions(block_order, first_row, row_count, block_rows):
    row_index = first_row + jnp.arange(row_count, dtype=jnp.int32)
    owner_block = row_index // block_rows
    block_ids = jnp.arange(block_order.shape[0], dtype=jnp.int32)
    picked = jnp.sum(
        jnp.where(owner_block[:, None] == block_ids[None, :], block_order[None, :], 0), axis=1
    )
    return picked * block_rows + row_index % block_rows


def rope_tables(positions, rotary_dims):
    half_rot = rotary_dims // 2
    frequency = jnp.exp(
        jnp.arange(half_rot, dtype=jnp.float32) * (-2.0 * math.log(10000.0) / rotary_dims)
    )
    angles = positions.astype(jnp.float32)[:, None] * frequency[None, :]
    angles = jnp.concatenate([angles, angles], axis=1)
    return (jnp.cos(angles), jnp.sin(angles))


def rotate(tensor, cosine, sine_table, rotary_dims):
    half_rot = rotary_dims // 2
    rotary_part = tensor[..., :rotary_dims]
    turned = jnp.concatenate([-rotary_part[..., half_rot:], rotary_part[..., :half_rot]], axis=-1)
    moved = rotary_part * cosine[:, None, :] + turned * sine_table[:, None, :]
    return jnp.concatenate([moved, tensor[..., rotary_dims:]], axis=-1)


def unrotate(incoming, cosine, sine_table, rotary_dims):
    half_rot = rotary_dims // 2
    rotary_part = incoming[..., :rotary_dims]
    scaled = rotary_part * sine_table[:, None, :]
    swapped = jnp.concatenate([scaled[..., half_rot:], -scaled[..., :half_rot]], axis=-1)
    moved = rotary_part * cosine[:, None, :] + swapped
    return jnp.concatenate([moved, incoming[..., rotary_dims:]], axis=-1)


def normalize(tensor, gain_row, shift_row):
    row_mean = jnp.mean(tensor, axis=-1, keepdims=True)
    centred = tensor - row_mean
    variance = jnp.mean(centred * centred, axis=-1, keepdims=True)
    inv_scale = lax.rsqrt(variance + norm_epsilon)
    unit_field = centred * inv_scale
    return (unit_field * gain_row + shift_row, unit_field, inv_scale)


def normalize_back(incoming, unit_field, inv_scale, gain_row):
    unit_grad = incoming * gain_row
    return inv_scale * (
        unit_grad
        - jnp.mean(unit_grad, axis=-1, keepdims=True)
        - unit_field * jnp.mean(unit_grad * unit_field, axis=-1, keepdims=True)
    )


def gelu_exact(argument):
    return 0.5 * argument * (1.0 + jax.scipy.special.erf(argument * root_half))


def gelu_slope(argument):
    return (
        0.5 * (1.0 + jax.scipy.special.erf(argument * root_half))
        + argument * jnp.exp(-0.5 * argument * argument) * inverse_root_two_pi
    )


def shards(
    stream_in,
    cotangent,
    ln_gain,
    ln_bias,
    w_qkv,
    b_qkv,
    w_out,
    out_bias,
    w_up,
    b_up,
    w_down,
    block_order,
):
    row_count = stream_in.shape[0]
    block_rows = row_count // 2
    head_count = w_out.shape[0] // HD
    inner_width = head_count * HD
    score_scale = HD ** (-0.5)
    own_start = lax.axis_index("ctx") * row_count
    positions = stored_positions(block_order, own_start, row_count, block_rows)
    cosine, sine_table = rope_tables(positions, ROT)
    normed_a, unit_a, scale_a = normalize(stream_in, ln_gain[0], ln_bias[0])
    normed_m, unit_m, scale_m = normalize(stream_in, ln_gain[1], ln_bias[1])
    attn_in = normed_a.astype(jnp.bfloat16)
    mlp_in = normed_m.astype(jnp.bfloat16)
    joined = (jnp.dot(attn_in, w_qkv, preferred_element_type=jnp.float32) + b_qkv).reshape(
        row_count, head_count, 3, HD
    )
    query_b = rotate(joined[:, :, 0], cosine, sine_table, ROT).astype(jnp.bfloat16)
    key_b = (
        rotate(joined[:, :, 1], cosine, sine_table, ROT)
        .astype(jnp.bfloat16)
        .reshape(row_count, inner_width)
    )
    value_b = joined[:, :, 2].astype(jnp.bfloat16).reshape(row_count, inner_width)
    running_max = jnp.full((head_count, row_count), masked_value, jnp.float32)
    accum = jnp.zeros((row_count, head_count, HD), jnp.float32)
    key_piece = lax.all_gather(key_b, "ctx", axis=0, tiled=True)
    value_piece = lax.all_gather(value_b, "ctx", axis=0, tiled=True)
    count_here = key_piece.shape[0]
    key_pos = stored_positions(block_order, jnp.int32(0), count_here, block_rows)
    key_heads = key_piece.reshape(count_here, head_count, HD)
    value_heads = value_piece.reshape(count_here, head_count, HD)
    scores = (
        jnp.einsum("qhd,khd->hqk", query_b, key_heads, preferred_element_type=jnp.float32)
        * score_scale
    )
    allowed = (key_pos[None, :] <= positions[:, None])[None]
    new_max = jnp.maximum(running_max, jnp.max(jnp.where(allowed, scores, masked_value), axis=2))
    weights = jnp.exp(jnp.where(allowed, scores - new_max[:, :, None], masked_value))
    rescale = jnp.exp(running_max - new_max)
    running_sum = jnp.sum(weights, axis=2)
    accum = accum * rescale.T[:, :, None] + jnp.einsum(
        "hqk,khd->qhd",
        weights.astype(jnp.bfloat16),
        value_heads,
        preferred_element_type=jnp.float32,
    )
    running_max, running_sum, accum = (new_max, running_sum, accum)
    log_total = running_max + jnp.log(running_sum)
    attn_out = (
        (accum / running_sum.T[:, :, None]).astype(jnp.bfloat16).reshape(row_count, inner_width)
    )
    hidden = jnp.dot(mlp_in, w_up, preferred_element_type=jnp.float32) + b_up
    gelu_out = gelu_exact(hidden).astype(jnp.bfloat16)
    branch_part = jnp.dot(attn_out, w_out, preferred_element_type=jnp.float32) + jnp.dot(
        gelu_out, w_down, preferred_element_type=jnp.float32
    )
    stream_out = (
        stream_in + out_bias + lax.psum(branch_part.astype(jnp.bfloat16), "tp").astype(jnp.float32)
    )
    cot_b = cotangent.astype(jnp.bfloat16)
    grad_down = jnp.einsum("rf,rd->fd", gelu_out, cot_b, preferred_element_type=jnp.float32)
    grad_out = jnp.einsum("re,rd->ed", attn_out, cot_b, preferred_element_type=jnp.float32)
    hidden_grad = jnp.einsum(
        "rd,fd->rf", cot_b, w_down, preferred_element_type=jnp.float32
    ) * gelu_slope(hidden)
    grad_bup = jnp.sum(hidden_grad, axis=0)
    hidden_b = hidden_grad.astype(jnp.bfloat16)
    grad_up = jnp.einsum("rd,rf->df", mlp_in, hidden_b, preferred_element_type=jnp.float32)
    mlp_back = jnp.einsum("rf,df->rd", hidden_b, w_up, preferred_element_type=jnp.float32)
    out_grad = jnp.einsum("rd,ed->re", cot_b, w_out, preferred_element_type=jnp.float32).astype(
        jnp.bfloat16
    )
    out_grad_heads = out_grad.reshape(row_count, head_count, HD)
    row_dot = jnp.sum(
        out_grad_heads.astype(jnp.float32)
        * attn_out.reshape(row_count, head_count, HD).astype(jnp.float32),
        axis=2,
    ).T

    def pair_terms(
        queries, query_pos, query_total, query_dot, query_grad, key_heads, key_pos, value_heads
    ):
        scores = (
            jnp.einsum("qhd,khd->hqk", queries, key_heads, preferred_element_type=jnp.float32)
            * score_scale
        )
        allowed = (key_pos[None, :] <= query_pos[:, None])[None]
        probability = jnp.exp(jnp.where(allowed, scores - query_total[:, :, None], masked_value))
        prob_grad = jnp.einsum(
            "qhd,khd->hqk", query_grad, value_heads, preferred_element_type=jnp.float32
        )
        score_grad = (probability * (prob_grad - query_dot[:, :, None]) * score_scale).astype(
            jnp.bfloat16
        )
        return (probability.astype(jnp.bfloat16), score_grad)

    key_piece = lax.all_gather(key_b, "ctx", axis=0, tiled=True)
    value_piece = lax.all_gather(value_b, "ctx", axis=0, tiled=True)
    count_here = key_piece.shape[0]
    key_pos = stored_positions(block_order, jnp.int32(0), count_here, block_rows)
    key_heads = key_piece.reshape(count_here, head_count, HD)
    value_heads = value_piece.reshape(count_here, head_count, HD)
    prob_b, score_b = pair_terms(
        query_b, positions, log_total, row_dot, out_grad_heads, key_heads, key_pos, value_heads
    )
    query_acc = jnp.einsum("hqk,khd->qhd", score_b, key_heads, preferred_element_type=jnp.float32)
    query_grad = query_acc
    total_all, dot_all = (
        lax.all_gather(log_total.T, "ctx", axis=0, tiled=True),
        lax.all_gather(row_dot.T, "ctx", axis=0, tiled=True),
    )
    own_keys = key_b.reshape(row_count, head_count, HD)
    own_values = value_b.reshape(row_count, head_count, HD)
    query_piece = lax.all_gather(query_b.reshape(row_count, inner_width), "ctx", axis=0, tiled=True)
    grad_piece = lax.all_gather(out_grad, "ctx", axis=0, tiled=True)
    count_here = query_piece.shape[0]
    query_pos = stored_positions(block_order, jnp.int32(0), count_here, block_rows)
    query_heads = query_piece.reshape(count_here, head_count, HD)
    grad_heads = grad_piece.reshape(count_here, head_count, HD)
    piece_total = total_all.T
    piece_dot = dot_all.T
    prob_b, score_b = pair_terms(
        query_heads, query_pos, piece_total, piece_dot, grad_heads, own_keys, positions, own_values
    )
    key_acc = jnp.einsum("hqk,qhd->khd", score_b, query_heads, preferred_element_type=jnp.float32)
    value_acc = jnp.einsum("hqk,qhd->khd", prob_b, grad_heads, preferred_element_type=jnp.float32)
    joined_grad = jnp.stack(
        [
            unrotate(query_grad, cosine, sine_table, ROT),
            unrotate(key_acc, cosine, sine_table, ROT),
            value_acc,
        ],
        axis=2,
    ).reshape(row_count, 3 * inner_width)
    grad_bqkv = jnp.sum(joined_grad, axis=0)
    joined_b = joined_grad.astype(jnp.bfloat16)
    grad_qkv = jnp.einsum("rd,re->de", attn_in, joined_b, preferred_element_type=jnp.float32)
    attn_back = jnp.einsum("re,de->rd", joined_b, w_qkv, preferred_element_type=jnp.float32)
    attn_total, mlp_total = (
        lax.psum(attn_back.astype(jnp.bfloat16), "tp").astype(jnp.float32),
        lax.psum(mlp_back.astype(jnp.bfloat16), "tp").astype(jnp.float32),
    )
    grad_in = (
        cotangent
        + normalize_back(attn_total, unit_a, scale_a, ln_gain[0])
        + normalize_back(mlp_total, unit_m, scale_m, ln_gain[1])
    )
    gain_grad = jnp.stack(
        [jnp.sum(attn_total * unit_a, axis=0), jnp.sum(mlp_total * unit_m, axis=0)]
    )
    shift_grad = jnp.stack([jnp.sum(attn_total, axis=0), jnp.sum(mlp_total, axis=0)])
    summed_qkv, summed_up = (
        lax.psum_scatter(
            grad_qkv.astype(jnp.bfloat16), "ctx", scatter_dimension=0, tiled=True
        ).astype(jnp.float32),
        lax.psum_scatter(
            grad_up.astype(jnp.bfloat16), "ctx", scatter_dimension=0, tiled=True
        ).astype(jnp.float32),
    )
    summed_out, summed_down = (
        lax.psum_scatter(
            grad_out.astype(jnp.bfloat16), "ctx", scatter_dimension=1, tiled=True
        ).astype(jnp.float32),
        lax.psum_scatter(
            grad_down.astype(jnp.bfloat16), "ctx", scatter_dimension=1, tiled=True
        ).astype(jnp.float32),
    )
    summed_small = (
        lax.psum(grad_bqkv.astype(jnp.bfloat16), "ctx").astype(jnp.float32),
        lax.psum(grad_bup.astype(jnp.bfloat16), "ctx").astype(jnp.float32),
        lax.psum(jnp.sum(cotangent, axis=0).astype(jnp.bfloat16), "ctx").astype(jnp.float32),
        lax.psum(gain_grad.astype(jnp.bfloat16), "ctx").astype(jnp.float32),
        lax.psum(shift_grad.astype(jnp.bfloat16), "ctx").astype(jnp.float32),
    )
    return (
        stream_out,
        grad_in,
        summed_qkv,
        summed_small[0],
        summed_out,
        summed_small[2],
        summed_up,
        summed_small[1],
        summed_down,
        summed_small[3],
        summed_small[4],
    )


def solution(mesh):
    placed = (
        P("ctx", None),
        P("ctx", None),
        P(),
        P(),
        P(None, "tp"),
        P("tp"),
        P("tp", None),
        P(),
        P(None, "tp"),
        P("tp"),
        P("tp", None),
        P(),
    )
    return jax.shard_map(
        shards,
        mesh=mesh,
        in_specs=placed,
        out_specs=(
            P("ctx", None),
            P("ctx", None),
            P("ctx", "tp"),
            P("tp"),
            P("tp", "ctx"),
            P(),
            P("ctx", "tp"),
            P("tp"),
            P("tp", "ctx"),
            P(),
            P(),
        ),
        check_vma=False,
    )
```

profile of v0, /device:TPU:0, one launch (start us, length us, event | category | flops | bytes accessed | tf_op | source)
XLA Modules:
  0.0 932.4 jit_solution(13913219721741613737)
XLA Ops:
  12.4 6.9 convolution_add_fusion
  51.9 7.4 multiply_convert_fusion.2
  59.3 9.1 fusion.100
  82.6 21.8 %all-gather.5.cloned.1.call-done = bf16[3072,512]{0,1:T(8,128)(2,1)} async-done(((bf16[384,512]{0,1:T(8,128)(2,1)}), bf16[3072,512]{0,1:T(8,128)(2,1)}) %all-gather.5.cloned.1.call-update) | async-done | bytes 3145744 | tf_op jit(solution)/shard_map/all_gather | solution.py:119
  112.4 54.9 %all-gather.7.cloned.1.call-done = bf16[3072,512]{0,1:T(8,128)(2,1)} async-done(((bf16[384,512]{0,1:T(8,128)(2,1)}), bf16[3072,512]{0,1:T(8,128)(2,1)}) %all-gather.7.cloned.1.call-update) | async-done | bytes 3145744 | tf_op jit(solution)/shard_map/all_gather | solution.py:120
  167.4 8.4 multiply_reduce_fusion.1
  175.8 11.4 %fusion.40 = f32[384,2,256]{2,0,1:T(8,128)} fusion(bf16[3072,2,256]{0,2,1:T(8,128)(2,1)} %bitcast.127, f32[2,384,3072]{2,1,0:T(8,128)} %copy-done.2, bf16[384,2,256]{0,2,1:T(8,128)(2,1)} %bitcast.106, bf16[3072,2,256]{0,2,1:T(8,128)(2,1)} %bitcast.129, f32[2,384]{1,0:T(2,128)S(1)} %bitcast.123, f32[2,384]{1,0:T(2,128)S(1)} %log_add_fusion, ...), kind=kOutput, calls=%fused_computation.67 | convolution fusion | flops 2432434176 | bytes 18094080 | tf_op jit(solution)/shard_map/hqk,khd->qhd/dot_general | solution.py:199
  189.5 31.1 %all_gather.25 = f32[3072,2]{0,1:T(2,128)S(1)} all-gather(f32[384,2]{0,1:T(2,128)S(1)} %get-tuple-element.61), channel_id=1, replica_groups=mesh['ctx'=8,'tp'=4] {'ctx'}, dimensions={0}, use_global_device_ids=true | all-gather | bytes 27648 | tf_op jit(solution)/shard_map/all_gather | solution.py:203
  220.7 31.0 %all_gather.23 = f32[3072,2]{0,1:T(2,128)S(1)} all-gather(f32[384,2]{0,1:T(2,128)S(1)} %get-tuple-element.55), channel_id=1, replica_groups=mesh['ctx'=8,'tp'=4] {'ctx'}, dimensions={0}, use_global_device_ids=true | all-gather | bytes 27648 | tf_op jit(solution)/shard_map/all_gather | solution.py:202
  251.7 8.1 fusion.101
  259.8 31.8 %all-gather.11.cloned.1.call-done = bf16[3072,512]{1,0:T(8,128)(2,1)} async-done(((bf16[384,512]{1,0:T(8,128)(2,1)}), bf16[3072,512]{1,0:T(8,128)(2,1)}) %all-gather.11.cloned.1.call-update) | async-done | bytes 3145744 | tf_op jit(solution)/shard_map/all_gather | solution.py:208
  296.2 13.1 %fusion.41 = f32[384,2,256]{2,0,1:T(8,128)} fusion(bf16[3072,2,256]{0,2,1:T(8,128)(2,1)} %bitcast.98, f32[2,3072,384]{2,1,0:T(8,128)} %fusion.101, bf16[3072,2,256]{0,2,1:T(8,128)(2,1)} %bitcast.95, f32[2,3072]{1,0:T(2,128)S(1)} %bitcast.118, f32[2,3072]{1,0:T(2,128)S(1)} %bitcast.116, pred[3072,384]{1,0:T(8,128)(4,1)} %broadcast_compare_fusion, ...), kind=kOutput, calls=%fused_computation.68 | convolution fusion | flops 2432434176 | bytes 18137088 | tf_op jit(solution)/shard_map/hqk,qhd->khd/dot_general | solution.py:218
  312.0 7.1 fusion.45
  326.2 7.1 convolution_convert_fusion.5
  339.6 10.7 %convolution_convert_fusion.1 = bf16[2048,2048]{1,0:T(8,128)(2,1)} fusion(bf16[384,2048]{1,0:T(8,128)(2,1)} %copy-done.24, f32[2048]{0:T(1024)S(1)} %bitcast.122, f32[2048]{0:T(1024)S(1)} %bitcast.112, f32[384,2048]{1,0:T(8,128)} %param.12, f32[384]{0:T(512)S(1)} %add_rsqrt_fusion, f32[384]{0:T(512)S(1)} %broadcast_multiply_fusion.5), kind=kOutput, calls=%fused_computation.6 | convolution fusion | flops 3229351936 | bytes 13126656 | tf_op jit(solution)/shard_map/rd,rf->df/dot_general | solution.py:161
  350.6 9.7 %convolution_convert_fusion = bf16[2048,2048]{1,0:T(8,128)(2,1)} fusion(bf16[384,2048]{1,0:T(8,128)(2,1)} %copy-done.23, bf16[384,2048]{1,0:T(8,128)(2,1)} %copy-done.14), kind=kOutput, calls=%fused_computation.5 | convolution fusion | flops 3225419776 | bytes 11534336 | tf_op jit(solution)/shard_map/rf,rd->fd/dot_general | solution.py:154
  360.4 8.5 convolution_convert_fusion.2
  370.5 57.9 %all-reduce.4.cloned.1.call-done = (bf16[384,2048]{1,0:T(8,128)(2,1)}, bf16[384,2048]{1,0:T(8,128)(2,1)}, bf16[384,2048]{1,0:T(8,128)(2,1)}) async-done(((bf16[384,2048]{1,0:T(8,128)(2,1)}, bf16[384,2048]{1,0:T(8,128)(2,1)}, bf16[384,2048]{1,0:T(8,128)(2,1)}), (bf16[384,2048]{1,0:T(8,128)(2,1)}, bf16[384,2048]{1,0:T(8,128)(2,1)}, bf16[384,2048]{1,0:T(8,128)(2,1)})) %all-reduce.4.cloned.1.call-update) | async-done | bytes 4718608 | tf_op jit(solution)/shard_map/psum | solution.py:151
  437.5 37.5 %all-reduce = (bf16[1536]{0:T(1024)(128)(2,1)S(1)}, bf16[2048]{0:T(1024)(128)(2,1)S(1)}, bf16[2048]{0:T(1024)(128)(2,1)S(1)}, bf16[2,2048]{1,0:T(2,128)(2,1)S(1)}, bf16[2,2048]{1,0:T(2,128)(2,1)S(1)}) all-reduce(bf16[1536]{0:T(1024)(128)(2,1)S(1)} %convert_element_type.179, ...), channel_id=1, replica_groups=mesh['ctx'=8,'tp'=4] {'ctx'}, use_global_device_ids=true, to_apply=%region_16.17 | all-reduce | flops 13824 | bytes 55296 | tf_op jit(solution)/shard_map/psum | solution.py:262
  478.0 7.0 fusion.24
  485.0 16.7 %reduce-scatter.7.cloned.1.call-done = bf16[512,256]{1,0:T(8,128)(2,1)} async-done(((bf16[512,2048]{1,0:T(8,128)(2,1)}), bf16[512,256]{1,0:T(8,128)(2,1)}) %reduce-scatter.7.cloned.1.call-update) | async-done | bytes 262160 | tf_op jit(solution)/shard_map/reduce_scatter | solution.py:254
  503.4 148.2 %reduce-scatter.9.cloned.1.call-done = bf16[256,2048]{1,0:T(8,128)(2,1)} async-done(((bf16[2048,2048]{1,0:T(8,128)(2,1)}), bf16[256,2048]{1,0:T(8,128)(2,1)}) %reduce-scatter.9.cloned.1.call-update) | async-done | bytes 1048592 | tf_op jit(solution)/shard_map/reduce_scatter | solution.py:249
  654.4 147.8 %reduce-scatter.11.cloned.1.call-done = bf16[2048,256]{1,0:T(8,128)(2,1)} async-done(((bf16[2048,2048]{1,0:T(8,128)(2,1)}), bf16[2048,256]{1,0:T(8,128)(2,1)}) %reduce-scatter.11.cloned.1.call-update) | async-done | bytes 1048592 | tf_op jit(solution)/shard_map/reduce_scatter | solution.py:257
  805.0 118.1 %reduce-scatter.5.cloned.1.call-done = bf16[256,1536]{1,0:T(8,128)(2,1)} async-done(((bf16[2048,1536]{1,0:T(8,128)(2,1)}), bf16[256,1536]{1,0:T(8,128)(2,1)}) %reduce-scatter.5.cloned.1.call-update) | async-done | bytes 786448 | tf_op jit(solution)/shard_map/reduce_scatter | solution.py:246
  (152 shorter events, 106.3 us)
Async XLA Ops:
  7.2 40.5 %copy-start = (bf16[512,2048]{1,0:T(8,128)(2,1)S(1)}, bf16[512,2048]{1,0:T(8,128)(2,1)}, u32[]{:S(2)}) copy-start(bf16[512,2048]{1,0:T(8,128)(2,1)} %param.18) | copy-start | bytes 6291460
  7.2 97.2 %all-gather.5.cloned.1.call-start = ((), (), s32[]{:S(2)}) async-start(), calls=%async_computation.4 | async-start | bytes 3538944 | tf_op jit(solution)/shard_map/all_gather | solution.py:119
  7.3 4.8 copy-start.18
  7.3 4.8 copy-start.21
  26.4 6.8 copy-start.20
  37.9 8.6 copy-start.5
  38.9 128.5 %all-gather.7.cloned.1.call-start = ((), (), s32[]{:S(2)}) async-start(), calls=%async_computation.5 | async-start | bytes 3538944 | tf_op jit(solution)/shard_map/all_gather | solution.py:120
  40.9 210.8 %all-gather.9.cloned.1.call-start = ((), (), s32[]{:S(2)}) async-start(), calls=%async_computation.6 | async-start | bytes 3538944 | tf_op jit(solution)/shard_map/all_gather | solution.py:207
  42.3 7.2 copy-start.13
  43.2 248.4 %all-gather.11.cloned.1.call-start = ((), (), s32[]{:S(2)}) async-start(), calls=%async_computation.7 | async-start | bytes 3538944 | tf_op jit(solution)/shard_map/all_gather | solution.py:208
  49.5 378.9 %all-reduce.4.cloned.1.call-start = ((), (), s32[]{:S(2)}) async-start(), calls=%async_computation.12 | async-start | bytes 9437184 | tf_op jit(solution)/shard_map/psum | solution.py:151
  51.8 23.2 %slice-start = ((s8[8388608]{0:T(1024)(128)(4,1)}), s8[4194304]{0:T(1024)(128)(4,1)S(1)}, s32[]{:S(2)}) async-start(s8[8388608]{0:T(1024)(128)(4,1)} %bitcast.124), calls=%async_computation.13 | async-start | bytes 8388608
  59.2 9.1 copy-start.23
  59.2 9.1 copy-start.15
  59.3 15.8 %slice-start.1 = ((s8[8388608]{0:T(1024)(128)(4,1)}), s8[4194304]{0:T(1024)(128)(4,1)S(1)}, s32[]{:S(2)}) async-start(s8[8388608]{0:T(1024)(128)(4,1)} %bitcast.124), calls=%async_computation.14 | async-start | bytes 8388608
  296.2 13.1 %copy-start.7 = (f32[384,2,256]{2,0,1:T(8,128)S(1)}, f32[384,2,256]{2,0,1:T(8,128)}, u32[]{:S(2)}) copy-start(f32[384,2,256]{2,0,1:T(8,128)} %fusion.40) | copy-start | bytes 2359300
  296.2 13.1 %copy-start.12 = (f32[384,64]{1,0:T(8,128)S(1)}, f32[384,64]{1,0:T(8,128)}, u32[]{:S(2)}) copy-start(f32[384,64]{1,0:T(8,128)} %copy-done.11) | copy-start | bytes 294916
  326.2 7.1 copy-start.4
  326.2 7.1 copy-start.16
  335.5 166.1 %reduce-scatter.7.cloned.1.call-start = ((), (), s32[]{:S(2)}) async-start(), calls=%async_computation.9 | async-start | bytes 2359296 | tf_op jit(solution)/shard_map/reduce_scatter | solution.py:254
  339.6 312.1 %reduce-scatter.9.cloned.1.call-start = ((), (), s32[]{:S(2)}) async-start(), calls=%async_computation.10 | async-start | bytes 9437184 | tf_op jit(solution)/shard_map/reduce_scatter | solution.py:249
  350.3 451.9 %reduce-scatter.11.cloned.1.call-start = ((), (), s32[]{:S(2)}) async-start(), calls=%async_computation.11 | async-start | bytes 9437184 | tf_op jit(solution)/shard_map/reduce_scatter | solution.py:257
  360.4 562.7 %reduce-scatter.5.cloned.1.call-start = ((), (), s32[]{:S(2)}) async-start(), calls=%async_computation.8 | async-start | bytes 7077888 | tf_op jit(solution)/shard_map/reduce_scatter | solution.py:246
  431.7 46.3 %copy-start.19 = (f32[2048]{0:T(1024)S(1)}, f32[2048]{0:T(1024)}, u32[]{:S(2)}) copy-start(f32[2048]{0:T(1024)} %param.19) | copy-start | bytes 24580
  (12 other events, 32.7 us)
Sparse Core Ops, SparseCore 0:
  39.0 65.3 all-gather.4
  106.5 60.8 all-gather.6
  169.4 61.2 all-gather.8
  233.3 58.2 all-gather.10
  335.6 92.6 all-reduce.3
  432.3 69.2 reduce-scatter.6
  505.3 146.3 reduce-scatter.8
  655.3 146.9 reduce-scatter.10
  805.8 117.1 reduce-scatter.4
where the time goes:
time: 939 us; the launch traced here: 932 us
  waiting for transfers between devices  597 us (64%)
  matrix products  131 us (14%)
  blocking collectives  99.6 us (11%)
  other arithmetic  56.1 us (6%)
  local copies, waits for them, and re-layouts  32.6 us (3%)
  between operations  14.8 us (2%)
    reduce_scatter x1, waiting for transfers between devices, shards(): lax.psum_scatter(grad_up.astype(jnp.bfloat16), 'ctx', scatter_dimension=0...  148 us
    reduce_scatter x1, waiting for transfers between devices, shards(): lax.psum_scatter(grad_down.astype(jnp.bfloat16), 'ctx', scatter_dimension...  148 us
    reduce_scatter x1, waiting for transfers between devices, shards(): lax.psum_scatter(grad_qkv.astype(jnp.bfloat16), 'ctx', scatter_dimension=...  118 us
    psum x1, waiting for transfers between devices, shards(): lax.psum(branch_part.astype(jnp.bfloat16), 'tp').astype(jnp.float32)  57.9 us
    all_gather x1, waiting for transfers between devices, shards(): value_piece = lax.all_gather(value_b, 'ctx', axis=0, tiled=True)  54.9 us
    psum x1, blocking collectives, shards(): lax.psum(grad_bqkv.astype(jnp.bfloat16), 'ctx').astype(jnp.float32)  37.5 us
    all_gather x1, waiting for transfers between devices, shards(): grad_piece = lax.all_gather(out_grad, 'ctx', axis=0, tiled=True)  31.8 us
    all_gather x1, blocking collectives, shards(): lax.all_gather(row_dot.T, 'ctx', axis=0, tiled=True)  31.1 us
  transfers between devices with their start and end apart: 9, of which 8 were waited for; matrix products, arithmetic and copies ran while one was open for 15% of the time, Pallas kernels for 0%

commit v1 on v0

--- a/solution.py
+++ b/solution.py
@@ -116,8 +116,11 @@
     value_b = joined[:, :, 2].astype(jnp.bfloat16).reshape(row_count, inner_width)
     running_max = jnp.full((head_count, row_count), masked_value, jnp.float32)
     accum = jnp.zeros((row_count, head_count, HD), jnp.float32)
-    key_piece = lax.all_gather(key_b, "ctx", axis=0, tiled=True)
-    value_piece = lax.all_gather(value_b, "ctx", axis=0, tiled=True)
+    key_piece, value_piece = jnp.split(
+        lax.all_gather(jnp.concatenate([key_b, value_b], axis=1), "ctx", axis=0, tiled=True),
+        [key_b.shape[1]],
+        axis=1,
+    )
     count_here = key_piece.shape[0]
     key_pos = stored_positions(block_order, jnp.int32(0), count_here, block_rows)
     key_heads = key_piece.reshape(count_here, head_count, HD)

time: 939 us -> 1060 us (1.13)
  waiting for transfers between devices: 597 us -> 719 us
    all_gather x0 -> x1, waiting for transfers between devices: none -> 96 us  [shards(): lax.all_gather(jnp.concatenate([key_b, value_b], axis=1), 'ctx', axis=0,...]
    all_gather x1, waiting for transfers between devices: 54.9 us -> 0.01 us  [shards(): value_piece = lax.all_gather(value_b, 'ctx', axis=0, tiled=True)]
    all_gather x1, waiting for transfers between devices: 21.8 us -> 55.5 us  [shards(): key_piece = lax.all_gather(key_b, 'ctx', axis=0, tiled=True)]
    all_gather x1, waiting for transfers between devices: 0.01 us -> 25.4 us  [shards(): lax.all_gather(query_b.reshape(row_count, inner_width), 'ctx', axis=0, ti...]
    all_gather x1, waiting for transfers between devices: 31.8 us -> 53.9 us  [shards(): grad_piece = lax.all_gather(out_grad, 'ctx', axis=0, tiled=True)]
  transfers between devices with their start and end apart: 9 -> 10, of which waited for: 8 -> 9; matrix products, arithmetic and copies ran while one was open for 15% -> 15% of each run, Pallas kernels for 0% -> 0%
where the time goes in v1:
time: 1060 us; the launch traced here: 1050 us
  waiting for transfers between devices  719 us (68%)
  matrix products  129 us (12%)
  blocking collectives  100 us (9%)
  other arithmetic  54.1 us (5%)
  local copies, waits for them, and re-layouts  34.7 us (3%)
  between operations  15.2 us (1%)
    reduce_scatter x1, waiting for transfers between devices, shards(): lax.psum_scatter(grad_up.astype(jnp.bfloat16), 'ctx', scatter_dimension=0...  148 us
    reduce_scatter x1, waiting for transfers between devices, shards(): lax.psum_scatter(grad_down.astype(jnp.bfloat16), 'ctx', scatter_dimension...  148 us
    reduce_scatter x1, waiting for transfers between devices, shards(): lax.psum_scatter(grad_qkv.astype(jnp.bfloat16), 'ctx', scatter_dimension=...  118 us
    all_gather x1, waiting for transfers between devices, shards(): lax.all_gather(jnp.concatenate([key_b, value_b], axis=1), 'ctx', axis=0,...  96 us
    psum x1, waiting for transfers between devices, shards(): lax.psum(branch_part.astype(jnp.bfloat16), 'tp').astype(jnp.float32)  56.4 us
    all_gather x1, waiting for transfers between devices, shards(): key_piece = lax.all_gather(key_b, 'ctx', axis=0, tiled=True)  55.5 us
    all_gather x1, waiting for transfers between devices, shards(): grad_piece = lax.all_gather(out_grad, 'ctx', axis=0, tiled=True)  53.9 us
    psum x1, blocking collectives, shards(): lax.psum(grad_bqkv.astype(jnp.bfloat16), 'ctx').astype(jnp.float32)  37.4 us
  transfers between devices with their start and end apart: 10, of which 9 were waited for; matrix products, arithmetic and copies ran while one was open for 15% of the time, Pallas kernels for 0%

profile of v1, /device:TPU:0, one launch (start us, length us, event | category | flops | bytes accessed | tf_op | source)
XLA Modules:
  0.0 1052.2 jit_solution(16733550251299761581)
XLA Ops:
  13.6 7.8 convolution_add_fusion
  51.9 7.4 multiply_convert_fusion.2
  75.6 25.4 %all-gather.12.cloned.1.call-done = bf16[3072,512]{0,1:T(8,128)(2,1)} async-done(((bf16[384,512]{0,1:T(8,128)(2,1)}), bf16[3072,512]{0,1:T(8,128)(2,1)}) %all-gather.12.cloned.1.call-update) | async-done | bytes 3145744 | tf_op jit(solution)/shard_map/all_gather | solution.py:210
  101.0 8.0 fusion.103
  109.0 55.5 %all-gather.8.cloned.1.call-done = bf16[3072,512]{0,1:T(8,128)(2,1)} async-done(((bf16[384,512]{0,1:T(8,128)(2,1)}), bf16[3072,512]{0,1:T(8,128)(2,1)}) %all-gather.8.cloned.1.call-update) | async-done | bytes 3145744 | tf_op jit(solution)/shard_map/all_gather | solution.py:193
  164.5 7.1 fusion.102
  171.6 53.9 %all-gather.14.cloned.1.call-done = bf16[3072,512]{1,0:T(8,128)(2,1)} async-done(((bf16[384,512]{1,0:T(8,128)(2,1)}), bf16[3072,512]{1,0:T(8,128)(2,1)}) %all-gather.14.cloned.1.call-update) | async-done | bytes 3145744 | tf_op jit(solution)/shard_map/all_gather | solution.py:211
  230.1 96.0 %all-gather.6.cloned.1.call-done = bf16[3072,1024]{0,1:T(8,128)(2,1)} async-done(((bf16[384,1024]{0,1:T(8,128)(2,1)}), bf16[3072,1024]{0,1:T(8,128)(2,1)}) %all-gather.6.cloned.1.call-update) | async-done | bytes 6291472 | tf_op jit(solution)/shard_map/all_gather | solution.py:120
  335.1 31.7 %all_gather.25 = f32[3072,2]{0,1:T(2,128)S(1)} all-gather(f32[384,2]{0,1:T(2,128)S(1)} %get-tuple-element.57), channel_id=1, replica_groups=mesh['ctx'=8,'tp'=4] {'ctx'}, dimensions={0}, use_global_device_ids=true | all-gather | bytes 27648 | tf_op jit(solution)/shard_map/all_gather | solution.py:205
  371.5 30.9 %all_gather.27 = f32[3072,2]{0,1:T(2,128)S(1)} all-gather(f32[384,2]{0,1:T(2,128)S(1)} %get-tuple-element.63), channel_id=1, replica_groups=mesh['ctx'=8,'tp'=4] {'ctx'}, dimensions={0}, use_global_device_ids=true | all-gather | bytes 27648 | tf_op jit(solution)/shard_map/all_gather | solution.py:206
  402.4 13.0 %fusion.41 = f32[384,2,256]{2,0,1:T(8,128)} fusion(bf16[3072,2,256]{0,2,1:T(8,128)(2,1)} %bitcast.106, f32[2,3072,384]{2,1,0:T(8,128)} %fusion.103, bf16[3072,2,256]{0,2,1:T(8,128)(2,1)} %bitcast.103, f32[2,3072]{1,0:T(2,128)S(1)} %bitcast.128, f32[2,3072]{1,0:T(2,128)S(1)} %bitcast.126, pred[3072,384]{1,0:T(8,128)(4,1)} %broadcast_compare_fusion, ...), kind=kOutput, calls=%fused_computation.68 | convolution fusion | flops 2432434176 | bytes 18137088 | tf_op jit(solution)/shard_map/hqk,qhd->khd/dot_general | solution.py:221
  417.7 8.3 fusion.45
  426.1 11.3 %fusion.40 = f32[384,2,256]{2,0,1:T(8,128)} fusion(bf16[3072,2,256]{0,2,1:T(8,128)(2,1)} %bitcast.110, f32[2,384,3072]{2,1,0:T(8,128)} %fusion.102, bf16[384,2,256]{0,2,1:T(8,128)(2,1)} %bitcast.116, bf16[3072,2,256]{0,2,1:T(8,128)(2,1)} %bitcast.138, f32[2,384]{1,0:T(2,128)S(1)} %bitcast.133, f32[2,384]{1,0:T(2,128)S(1)} %log_add_fusion, ...), kind=kOutput, calls=%fused_computation.67 | convolution fusion | flops 2432434176 | bytes 18094080 | tf_op jit(solution)/shard_map/hqk,khd->qhd/dot_general | solution.py:202
  446.6 7.1 convolution_convert_fusion.5
  460.1 10.4 convolution_convert_fusion.1
  470.8 9.7 convolution_convert_fusion
  481.1 8.7 convolution_convert_fusion.2
  491.4 56.4 %all-reduce.4.cloned.1.call-done = (bf16[384,2048]{1,0:T(8,128)(2,1)}, bf16[384,2048]{1,0:T(8,128)(2,1)}, bf16[384,2048]{1,0:T(8,128)(2,1)}) async-done(((bf16[384,2048]{1,0:T(8,128)(2,1)}, bf16[384,2048]{1,0:T(8,128)(2,1)}, bf16[384,2048]{1,0:T(8,128)(2,1)}), (bf16[384,2048]{1,0:T(8,128)(2,1)}, bf16[384,2048]{1,0:T(8,128)(2,1)}, bf16[384,2048]{1,0:T(8,128)(2,1)})) %all-reduce.4.cloned.1.call-update) | async-done | bytes 4718608 | tf_op jit(solution)/shard_map/psum | solution.py:154
  556.9 37.4 %all-reduce = (bf16[1536]{0:T(1024)(128)(2,1)S(1)}, bf16[2048]{0:T(1024)(128)(2,1)S(1)}, bf16[2048]{0:T(1024)(128)(2,1)S(1)}, bf16[2,2048]{1,0:T(2,128)(2,1)S(1)}, bf16[2,2048]{1,0:T(2,128)(2,1)S(1)}) all-reduce(bf16[1536]{0:T(1024)(128)(2,1)S(1)} %convert_element_type.179, ...), channel_id=1, replica_groups=mesh['ctx'=8,'tp'=4] {'ctx'}, use_global_device_ids=true, to_apply=%region_16.17 | all-reduce | flops 13824 | bytes 55296 | tf_op jit(solution)/shard_map/psum | solution.py:265
  597.4 7.0 fusion.24
  604.3 16.9 %reduce-scatter.7.cloned.1.call-done = bf16[512,256]{1,0:T(8,128)(2,1)} async-done(((bf16[512,2048]{1,0:T(8,128)(2,1)}), bf16[512,256]{1,0:T(8,128)(2,1)}) %reduce-scatter.7.cloned.1.call-update) | async-done | bytes 262160 | tf_op jit(solution)/shard_map/reduce_scatter | solution.py:257
  623.0 148.3 %reduce-scatter.9.cloned.1.call-done = bf16[256,2048]{1,0:T(8,128)(2,1)} async-done(((bf16[2048,2048]{1,0:T(8,128)(2,1)}), bf16[256,2048]{1,0:T(8,128)(2,1)}) %reduce-scatter.9.cloned.1.call-update) | async-done | bytes 1048592 | tf_op jit(solution)/shard_map/reduce_scatter | solution.py:252
  774.0 147.8 %reduce-scatter.11.cloned.1.call-done = bf16[2048,256]{1,0:T(8,128)(2,1)} async-done(((bf16[2048,2048]{1,0:T(8,128)(2,1)}), bf16[2048,256]{1,0:T(8,128)(2,1)}) %reduce-scatter.11.cloned.1.call-update) | async-done | bytes 1048592 | tf_op jit(solution)/shard_map/reduce_scatter | solution.py:260
  924.6 117.9 %reduce-scatter.5.cloned.1.call-done = bf16[256,1536]{1,0:T(8,128)(2,1)} async-done(((bf16[2048,1536]{1,0:T(8,128)(2,1)}), bf16[256,1536]{1,0:T(8,128)(2,1)}) %reduce-scatter.5.cloned.1.call-update) | async-done | bytes 786448 | tf_op jit(solution)/shard_map/reduce_scatter | solution.py:249
  (183 shorter events, 113.1 us)
Async XLA Ops:
  7.2 35.6 %copy-start = (bf16[512,2048]{1,0:T(8,128)(2,1)S(1)}, bf16[512,2048]{1,0:T(8,128)(2,1)}, u32[]{:S(2)}) copy-start(bf16[512,2048]{1,0:T(8,128)(2,1)} %param.18) | copy-start | bytes 6291460
  7.2 93.8 %all-gather.12.cloned.1.call-start = ((), (), s32[]{:S(2)}) async-start(), calls=%async_computation.7 | async-start | bytes 3538944 | tf_op jit(solution)/shard_map/all_gather | solution.py:210
  8.2 43.7 %copy-start.25 = (f32[1,2048]{1,0:T(1,128)}, f32[1,2048]{1,0:T(1,128)S(1)}, u32[]{:S(2)}) copy-start(f32[1,2048]{1,0:T(1,128)S(1)} %get-tuple-element.56) | copy-start | bytes 24580
  34.5 7.1 copy-start.5
  35.5 129.0 %all-gather.8.cloned.1.call-start = ((), (), s32[]{:S(2)}) async-start(), calls=%async_computation.5 | async-start | bytes 3538944 | tf_op jit(solution)/shard_map/all_gather | solution.py:193
  36.8 7.8 copy-start.7
  37.8 187.7 %all-gather.14.cloned.1.call-start = ((), (), s32[]{:S(2)}) async-start(), calls=%async_computation.8 | async-start | bytes 3538944 | tf_op jit(solution)/shard_map/all_gather | solution.py:211
  44.6 281.5 %all-gather.6.cloned.1.call-start = ((), (), s32[]{:S(2)}) async-start(), calls=%async_computation.4 | async-start | bytes 7077888 | tf_op jit(solution)/shard_map/all_gather | solution.py:120
  46.0 5.9 copy-start.32
  47.0 379.0 %all-gather.10.cloned.1.call-start = ((), (), s32[]{:S(2)}) async-start(), calls=%async_computation.6 | async-start | bytes 3538944 | tf_op jit(solution)/shard_map/all_gather | solution.py:194
  47.6 500.2 %all-reduce.4.cloned.1.call-start = ((), (), s32[]{:S(2)}) async-start(), calls=%async_computation.13 | async-start | bytes 9437184 | tf_op jit(solution)/shard_map/psum | solution.py:154
  48.9 10.3 slice-start
  51.9 7.4 slice-start.1
  51.9 18.9 %slice-start.2 = ((s8[8388608]{0:T(1024)(128)(4,1)}), s8[4194304]{0:T(1024)(128)(4,1)S(1)}, s32[]{:S(2)}) async-start(s8[8388608]{0:T(1024)(128)(4,1)} %bitcast.136), calls=%async_computation.16 | async-start | bytes 8388608
  59.3 11.4 %slice-start.3 = ((s8[8388608]{0:T(1024)(128)(4,1)}), s8[4194304]{0:T(1024)(128)(4,1)S(1)}, s32[]{:S(2)}) async-start(s8[8388608]{0:T(1024)(128)(4,1)} %bitcast.136), calls=%async_computation.17 | async-start | bytes 8388608
  332.2 34.6 %copy-start.20 = (bf16[384,512]{0,1:T(8,128)(2,1)S(1)}, bf16[384,512]{0,1:T(8,128)(2,1)}, u32[]{:S(2)}) copy-start(bf16[384,512]{0,1:T(8,128)(2,1)} %copy.89) | copy-start | bytes 1179652
  417.7 8.4 copy-start.29
  446.6 7.1 copy-start.4
  446.6 7.1 copy-start.19
  455.9 165.3 %reduce-scatter.7.cloned.1.call-start = ((), (), s32[]{:S(2)}) async-start(), calls=%async_computation.10 | async-start | bytes 2359296 | tf_op jit(solution)/shard_map/reduce_scatter | solution.py:257
  460.0 311.3 %reduce-scatter.9.cloned.1.call-start = ((), (), s32[]{:S(2)}) async-start(), calls=%async_computation.11 | async-start | bytes 9437184 | tf_op jit(solution)/shard_map/reduce_scatter | solution.py:252
  470.5 451.4 %reduce-scatter.11.cloned.1.call-start = ((), (), s32[]{:S(2)}) async-start(), calls=%async_computation.12 | async-start | bytes 9437184 | tf_op jit(solution)/shard_map/reduce_scatter | solution.py:260
  480.5 562.0 %reduce-scatter.5.cloned.1.call-start = ((), (), s32[]{:S(2)}) async-start(), calls=%async_computation.9 | async-start | bytes 7077888 | tf_op jit(solution)/shard_map/reduce_scatter | solution.py:249
  551.1 46.3 %copy-start.22 = (f32[2048]{0:T(1024)S(1)}, f32[2048]{0:T(1024)}, u32[]{:S(2)}) copy-start(f32[2048]{0:T(1024)} %param.19) | copy-start | bytes 24580
  (25 other events, 73.7 us)
Sparse Core Ops, SparseCore 0:
  35.6 65.3 all-gather.11
  103.6 60.8 all-gather.7
  167.3 58.1 all-gather.13
  228.0 98.1 all-gather.5
  328.1 61.2 all-gather.9
  456.0 91.6 all-reduce.3
  551.9 69.3 reduce-scatter.6
  624.9 146.3 reduce-scatter.8
  774.9 146.9 reduce-scatter.10
  925.3 117.1 reduce-scatter.4
